TPU v7x, 128 devices: a whole 4x4x4 slice. The times are simulated.
128 devices in a mesh: replica: 16 (over z, y), model: 8 (over x, core).
Axes of the slice: x: 4, y: 4, z: 4, core: 2. Of those that a mesh axis runs over, the one named last changes fastest.
Arguments:
- slope_up: float32 [16, 1024, 4096], P('replica', None, 'model'), may hold values from -4 to 4
- slope_down: float32 [16, 4096, 1024], P('replica', 'model'), may hold values from -4 to 4
- slope_query: float32 [16, 1024, 1024], P('replica', None, 'model'), may hold values from -4 to 4
- slope_key: float32 [16, 1024, 1024], P('replica', None, 'model'), may hold values from -4 to 4
- slope_value: float32 [16, 1024, 1024], P('replica', None, 'model'), may hold values from -4 to 4
- slope_mixed: float32 [16, 1024, 1024], P('replica', 'model'), may hold values from -4 to 4
- slope_norm: float32 [16, 1024], P('replica'), may hold values from -8 to 8
- slope_bias: float32 [16, 1024], P('replica'), may hold values from -8 to 8
- param_up: float32 [1024, 4096], P('replica', 'model'), may hold values from -0.25 to 0.25
- param_down: float32 [4096, 1024], P('model', 'replica'), may hold values from -0.125 to 0.125
- param_query: float32 [1024, 1024], P('replica', 'model'), may hold values from -0.25 to 0.25
- param_key: float32 [1024, 1024], P('replica', 'model'), may hold values from -0.25 to 0.25
- param_value: float32 [1024, 1024], P('replica', 'model'), may hold values from -0.25 to 0.25
- param_mixed: float32 [1024, 1024], P('model', 'replica'), may hold values from -0.25 to 0.25
- param_norm: float32 [1024], P('replica'), may hold values from 0.25 to 1.75
- param_bias: float32 [1024], P('replica'), may hold values from -3 to 3
- state_up: float32 [1024, 4096], P('replica', 'model'), may hold values from 0.0001953125 to 0.001953125
- state_down: float32 [4096, 1024], P('model', 'replica'), may hold values from 4.8828126e-05 to 0.00048828125
- state_query: float32 [1024, 1024], P('replica', 'model'), may hold values from 0.0001953125 to 0.001953125
- state_key: float32 [1024, 1024], P('replica', 'model'), may hold values from 0.0001953125 to 0.001953125
- state_value: float32 [1024, 1024], P('replica', 'model'), may hold values from 0.0001953125 to 0.001953125
- state_mixed: float32 [1024, 1024], P('model', 'replica'), may hold values from 0.0001953125 to 0.001953125
- state_norm: float32 [1024], P('replica'), may hold values from 0.05 to 0.8
- state_bias: float32 [1024], P('replica'), may hold values from 0.05 to 0.8
Outputs:
- half_up: bfloat16 [1024, 4096], P(None, 'model')
- half_down: bfloat16 [4096, 1024], P('model')
- half_query: bfloat16 [1024, 1024], P(None, 'model')
- half_key: bfloat16 [1024, 1024], P(None, 'model')
- half_value: bfloat16 [1024, 1024], P(None, 'model')
- half_mixed: bfloat16 [1024, 1024], P('model')
- half_norm: bfloat16 [1024], replicated
- half_bias: bfloat16 [1024], replicated
- next_up: float32 [1024, 4096], P('replica', 'model')
- next_down: float32 [4096, 1024], P('model', 'replica')
- next_query: float32 [1024, 1024], P('replica', 'model')
- next_key: float32 [1024, 1024], P('replica', 'model')
- next_value: float32 [1024, 1024], P('replica', 'model')
- next_mixed: float32 [1024, 1024], P('model', 'replica')
- next_norm: float32 [1024], P('replica')
- next_bias: float32 [1024], P('replica')
- state_new_up: float32 [1024, 4096], P('replica', 'model')
- state_new_down: float32 [4096, 1024], P('model', 'replica')
- state_new_query: float32 [1024, 1024], P('replica', 'model')
- state_new_key: float32 [1024, 1024], P('replica', 'model')
- state_new_value: float32 [1024, 1024], P('replica', 'model')
- state_new_mixed: float32 [1024, 1024], P('model', 'replica')
- state_new_norm: float32 [1024], P('replica')
- state_new_bias: float32 [1024], P('replica')
All inputs are finite; a program needn't handle non-finite values.
Results may differ from a plain program's by a relative error of at most 0.001.
Values may be sent and summed in bfloat16 or wider, within the bound.
No kernel may reach another device: no remote copies, remote signals or barrier semaphores. Data moves between devices by JAX's collectives and lax.ppermute only.
A program may use at most 64 MiB of HBM per device.

v0:
```python
import jax
import jax.numpy as jnp
from jax import lax
from jax.sharding import PartitionSpec as P

learn_rate = 0.025
hold_rate = 0.7


def split_up(x, dim, length):
    before, after = (x.shape[:dim], x.shape[dim + 1 :])
    return jnp.moveaxis(x.reshape(*before, length, -1, *after), dim, 0)


def one_scatter(arrays, axis, dims):
    length = lax.axis_size(axis)
    parts = [split_up(a, dim, length) for a, dim in zip(arrays, dims)]
    lines = jnp.concatenate([b.reshape(length, -1) for b in parts], axis=1)
    rows = max(16, -(-lines.shape[1] // 1024) * 8)
    lines = jnp.pad(lines, ((0, 0), (0, rows * 128 - lines.shape[1]))).reshape(-1, 128)
    line, at, finished = (lax.psum_scatter(lines, axis, tiled=True).reshape(-1), 0, [])
    for b in parts:
        part = b[0]
        finished.append(line[at : at + part.size].reshape(part.shape))
        at += part.size
    return tuple(finished)


def from_everyone(x, axis):
    copies = jnp.broadcast_to(x, (lax.axis_size(axis), *x.shape))
    return lax.all_to_all(copies, axis, split_axis=0, concat_axis=0, tiled=True)


def taken_together(x, axis):
    return from_everyone(x, axis).sum(axis=0)


def together(arrays, axis):
    ends = [0]
    for a in arrays:
        ends.append(ends[-1] + a.size)
    subtotal = taken_together(jnp.concatenate([a.ravel() for a in arrays]), axis)
    return tuple((subtotal[b:e].reshape(a.shape) for a, b, e in zip(arrays, ends, ends[1:])))


def rows_first(arrays, axis, dims):
    turned = [jnp.moveaxis(a, dim, 0) for a, dim in zip(arrays, dims)]
    both = jnp.concatenate([t.reshape(len(t), -1) for t in turned], axis=1)
    whole, at, finished = (lax.all_gather(both, axis, axis=0, tiled=True), 0, [])
    for t, dim in zip(turned, dims):
        section = whole[:, at : at + t[0].size].reshape(-1, *t.shape[1:])
        finished.append(jnp.moveaxis(section, 0, dim))
        at += t[0].size
    return tuple(finished)


def local(
    slope_up,
    slope_down,
    slope_query,
    slope_key,
    slope_value,
    slope_mixed,
    slope_norm,
    slope_bias,
    param_up,
    param_down,
    param_query,
    param_key,
    param_value,
    param_mixed,
    param_norm,
    param_bias,
    state_up,
    state_down,
    state_query,
    state_key,
    state_value,
    state_mixed,
    state_norm,
    state_bias,
):
    mean_up, mean_down, mean_query, mean_key, mean_value, mean_mixed, mean_norm, mean_bias = (
        one_scatter(
            (
                slope_up[0],
                slope_down[0],
                slope_query[0],
                slope_key[0],
                slope_value[0],
                slope_mixed[0],
                slope_norm[0],
                slope_bias[0],
            ),
            "replica",
            (0, 1, 0, 0, 0, 1, 0, 0),
        )
    )
    mean_rate = lax.axis_size("replica") ** (-0.5)
    mean_up = mean_up * mean_rate
    mean_down = mean_down * mean_rate
    mean_query = mean_query * mean_rate
    mean_key = mean_key * mean_rate
    mean_value = mean_value * mean_rate
    mean_mixed = mean_mixed * mean_rate
    mean_norm = mean_norm * mean_rate
    mean_bias = mean_bias * mean_rate
    (
        own_up,
        own_down,
        own_query,
        own_key,
        own_value,
        own_mixed,
        slope_up_norm,
        slope_down_norm,
        slope_query_norm,
        slope_key_norm,
        slope_value_norm,
        slope_mixed_norm,
    ) = together(
        (
            jnp.sum(param_up * param_up, axis=1, keepdims=True),
            jnp.sum(param_down * param_down, axis=0, keepdims=True),
            jnp.sum(param_query * param_query, axis=1, keepdims=True),
            jnp.sum(param_key * param_key, axis=1, keepdims=True),
            jnp.sum(param_value * param_value, axis=1, keepdims=True),
            jnp.sum(param_mixed * param_mixed, axis=0, keepdims=True),
            jnp.sum(mean_up * mean_up, axis=1, keepdims=True),
            jnp.sum(mean_down * mean_down, axis=0, keepdims=True),
            jnp.sum(mean_query * mean_query, axis=1, keepdims=True),
            jnp.sum(mean_key * mean_key, axis=1, keepdims=True),
            jnp.sum(mean_value * mean_value, axis=1, keepdims=True),
            jnp.sum(mean_mixed * mean_mixed, axis=0, keepdims=True),
        ),
        "model",
    )
    mean_up = mean_up * (jnp.sqrt(own_up) * lax.rsqrt(slope_up_norm + 1e-06))
    mean_down = mean_down * (jnp.sqrt(own_down) * lax.rsqrt(slope_down_norm + 1e-06))
    mean_query = mean_query * (jnp.sqrt(own_query) * lax.rsqrt(slope_query_norm + 1e-06))
    mean_key = mean_key * (jnp.sqrt(own_key) * lax.rsqrt(slope_key_norm + 1e-06))
    mean_value = mean_value * (jnp.sqrt(own_value) * lax.rsqrt(slope_value_norm + 1e-06))
    mean_mixed = mean_mixed * (jnp.sqrt(own_mixed) * lax.rsqrt(slope_mixed_norm + 1e-06))
    state_new_up = hold_rate * state_up + (1.0 - hold_rate) * mean_up * mean_up
    next_up = param_up - learn_rate * mean_up * lax.rsqrt(state_new_up + 1e-06)
    state_new_down = hold_rate * state_down + (1.0 - hold_rate) * mean_down * mean_down
    next_down = param_down - learn_rate * mean_down * lax.rsqrt(state_new_down + 1e-06)
    state_new_query = hold_rate * state_query + (1.0 - hold_rate) * mean_query * mean_query
    next_query = param_query - learn_rate * mean_query * lax.rsqrt(state_new_query + 1e-06)
    state_new_key = hold_rate * state_key + (1.0 - hold_rate) * mean_key * mean_key
    next_key = param_key - learn_rate * mean_key * lax.rsqrt(state_new_key + 1e-06)
    state_new_value = hold_rate * state_value + (1.0 - hold_rate) * mean_value * mean_value
    next_value = param_value - learn_rate * mean_value * lax.rsqrt(state_new_value + 1e-06)
    state_new_mixed = hold_rate * state_mixed + (1.0 - hold_rate) * mean_mixed * mean_mixed
    next_mixed = param_mixed - learn_rate * mean_mixed * lax.rsqrt(state_new_mixed + 1e-06)
    state_new_norm = hold_rate * state_norm + (1.0 - hold_rate) * mean_norm * mean_norm
    next_norm = param_norm - learn_rate * mean_norm * lax.rsqrt(state_new_norm + 1e-06)
    state_new_bias = hold_rate * state_bias + (1.0 - hold_rate) * mean_bias * mean_bias
    next_bias = param_bias - learn_rate * mean_bias * lax.rsqrt(state_new_bias + 1e-06)
    half_up, half_down, half_query, half_key, half_value, half_mixed, half_norm, half_bias = (
        rows_first(
            (
                next_up.astype(jnp.bfloat16),
                next_down.astype(jnp.bfloat16),
                next_query.astype(jnp.bfloat16),
                next_key.astype(jnp.bfloat16),
                next_value.astype(jnp.bfloat16),
                next_mixed.astype(jnp.bfloat16),
                next_norm.astype(jnp.bfloat16),
                next_bias.astype(jnp.bfloat16),
            ),
            "replica",
            (0, 1, 0, 0, 0, 1, 0, 0),
        )
    )
    return (
        half_up,
        half_down,
        half_query,
        half_key,
        half_value,
        half_mixed,
        half_norm,
        half_bias,
        next_up,
        next_down,
        next_query,
        next_key,
        next_value,
        next_mixed,
        next_norm,
        next_bias,
        state_new_up,
        state_new_down,
        state_new_query,
        state_new_key,
        state_new_value,
        state_new_mixed,
        state_new_norm,
        state_new_bias,
    )


def solution(mesh):
    placed = (
        P("replica", None, "model"),
        P("replica", "model", None),
        P("replica", None, "model"),
        P("replica", None, "model"),
        P("replica", None, "model"),
        P("replica", "model", None),
        P("replica", None),
        P("replica", None),
        P("replica", "model"),
        P("model", "replica"),
        P("replica", "model"),
        P("replica", "model"),
        P("replica", "model"),
        P("model", "replica"),
        P("replica"),
        P("replica"),
        P("replica", "model"),
        P("model", "replica"),
        P("replica", "model"),
        P("replica", "model"),
        P("replica", "model"),
        P("model", "replica"),
        P("replica"),
        P("replica"),
    )
    return jax.shard_map(
        local,
        mesh=mesh,
        in_specs=placed,
        out_specs=(
            P(None, "model"),
            P("model", None),
            P(None, "model"),
            P(None, "model"),
            P(None, "model"),
            P("model", None),
            P(),
            P(),
            P("replica", "model"),
            P("model", "replica"),
            P("replica", "model"),
            P("replica", "model"),
            P("replica", "model"),
            P("model", "replica"),
            P("replica"),
            P("replica"),
            P("replica", "model"),
            P("model", "replica"),
            P("replica", "model"),
            P("replica", "model"),
            P("replica", "model"),
            P("model", "replica"),
            P("replica"),
            P("replica"),
        ),
        check_vma=False,
    )
```

profile of v0, /device:TPU:1, one launch (start us, length us, event | category | flops | bytes accessed | tf_op | source)
XLA Modules:
  0.0 255.1 jit_solution(3883371217189918573)
XLA Ops:
  7.2 1.8 reshape_reshape_squeeze.12
  9.0 1.4 constant_dynamic-update-slice_fusion.5
  10.4 1.9 copy.120
  12.4 2.7 %copy.121 = f32[16,512,64]{2,1,0:T(8,128)} copy(f32[16,512,64]{1,2,0:T(8,128)S(1)} %bitcast.21) | data formatting | bytes 4194304 | tf_op jit(solution)/shard_map/transpose | solution.py:12
  15.1 2.9 %reshape.143 = f32[16,32768]{1,0:T(8,128)S(1)} reshape(f32[16,512,64]{2,1,0:T(8,128)} %copy.121) | data formatting | bytes 4194304 | tf_op jit(solution)/shard_map/reshape | solution.py:18
  19.8 1.9 reshape_reshape_squeeze.15
  21.8 2.1 copy.122
  23.8 1.4 copy.123
  28.4 1.4 constant_dynamic-update-slice_fusion.4
  29.8 1.9 constant_dynamic-update-slice_fusion.3
  31.7 1.9 constant_dynamic-update-slice_fusion.2
  35.2 1.3 dynamic-update-slice.6
  36.5 1.4 dynamic-update-slice.7
  37.9 5.9 %pad.4 = f32[16,99328]{1,0:T(8,128)} pad(f32[16,98432]{1,0:T(8,128)} %dynamic-update-slice.7, f32[]{:T(128)} %constant.8.clone.1), padding=0_0x0_896 | pad | bytes 12656644 | tf_op jit(solution)/shard_map/jit(_pad)/pad | solution.py:20
  43.7 5.0 %reshape.145 = f32[12416,128]{1,0:T(8,128)} reshape(f32[16,99328]{1,0:T(8,128)} %pad.4) | data formatting | bytes 12713984 | tf_op jit(solution)/shard_map/reshape | solution.py:20
  51.3 123.8 %all-reduce.4.cloned.1.call-done = f32[12416,128]{1,0:T(8,128)} async-done(((f32[12416,128]{1,0:T(8,128)}), f32[12416,128]{1,0:T(8,128)}) %all-reduce.4.cloned.1.call-update) | async-done | bytes 6357008
  178.4 5.1 %all-to-all-start = ((f32[8,1,768]{2,1,0:T(1,128)}), f32[8,1,768]{2,1,0:T(1,128)S(1)}, u32[]{:S(2)}, u32[]{:S(2)}) async-start(f32[8,1,768]{2,1,0:T(1,128)} %broadcast_in_dim.3), calls=%async_computation | async-start | bytes 49152 | tf_op jit(solution)/shard_map/all_to_all | solution.py:31
  185.6 2.6 %all-to-all-done = f32[8,1,768]{2,1,0:T(1,128)S(1)} async-done(((f32[8,1,768]{2,1,0:T(1,128)}), f32[8,1,768]{2,1,0:T(1,128)S(1)}, u32[]{:S(2)}, u32[]{:S(2)}) %all-to-all-start) | async-done | bytes 24608 | tf_op jit(solution)/shard_map/all_to_all | solution.py:31
  190.6 1.6 fusion.7
  193.1 46.4 %all-gather.2.cloned.1.call-done = bf16[1024,1538]{1,0:T(8,128)(2,1)} async-done(((bf16[64,1538]{1,0:T(8,128)(2,1)}), bf16[1024,1538]{1,0:T(8,128)(2,1)}) %all-gather.2.cloned.1.call-update) | async-done | bytes 3149840 | tf_op jit(solution)/shard_map/all_gather | solution.py:49
  239.5 2.7 %slice_bitcast_fusion = (bf16[512,1024]{0,1:T(8,128)(2,1)S(1)}, bf16[1024,512]{1,0:T(8,128)(2,1)}) fusion(bf16[1024,1538]{1,0:T(8,128)(2,1)} %all-gather.2.cloned.1.call-done), kind=kLoop, calls=%fused_computation | loop fusion | bytes 4194304 | tf_op jit(solution)/shard_map/transpose | solution.py:52
  242.1 1.3 copy.129
  243.4 2.1 slice_bitcast_fusion.1
  246.4 1.9 slice_reduce_fusion
  (90 shorter events, 17.8 us)
Async XLA Ops:
  7.2 167.8 %all-reduce.4.cloned.1.call-start = ((), (), s32[]{:S(2)}) async-start(), calls=%async_computation.2 | async-start | bytes 12713984
  12.4 5.7 %copy-start.4 = (f32[1,1024,128]{2,1,0:T(8,128)S(1)}, f32[1,1024,128]{2,1,0:T(8,128)}, u32[]{:S(2)}) copy-start(f32[1,1024,128]{2,1,0:T(8,128)} %param.26) | copy-start | bytes 1572868
  12.4 6.6 %copy-start.5 = (f32[1,1024,128]{2,1,0:T(8,128)S(1)}, f32[1,1024,128]{2,1,0:T(8,128)}, u32[]{:S(2)}) copy-start(f32[1,1024,128]{2,1,0:T(8,128)} %param.27) | copy-start | bytes 1572868
  15.1 11.8 %copy-start.16 = (f32[1,1024]{1,0:T(1,128)S(1)}, f32[1,1024]{1,0:T(1,128)}, u32[]{:S(2)}) copy-start(f32[1,1024]{1,0:T(1,128)} %param.30) | copy-start | bytes 12292
  15.1 12.5 %copy-start.17 = (f32[1,1024]{1,0:T(1,128)S(1)}, f32[1,1024]{1,0:T(1,128)}, u32[]{:S(2)}) copy-start(f32[1,1024]{1,0:T(1,128)} %param.31) | copy-start | bytes 12292
  26.4 7.2 %copy-start.1 = (f32[16,8192]{1,0:T(8,128)S(1)}, f32[16,8192]{1,0:T(8,128)}, u32[]{:S(2)}) copy-start(f32[16,8192]{1,0:T(8,128)} %reshape_reshape_squeeze.15) | copy-start | bytes 1572868
  26.4 8.0 %copy-start = (f32[16,8192]{1,0:T(8,128)S(1)}, f32[16,8192]{1,0:T(8,128)}, u32[]{:S(2)}) copy-start(f32[16,8192]{1,0:T(8,128)} %reshape.144) | copy-start | bytes 1572868
  48.8 2.0 copy-start.11
  48.8 2.1 copy-start.9
  48.8 2.1 copy-start.10
  48.8 2.2 copy-start.2
  48.8 2.3 copy-start.3
  48.8 135.7 %copy-start.18 = (f32[64]{0:T(128)S(1)}, f32[64]{0:T(128)}, u32[]{:S(2)}) copy-start(f32[64]{0:T(128)} %param.39) | copy-start | bytes 772
  48.8 135.7 %copy-start.19 = (f32[64]{0:T(128)S(1)}, f32[64]{0:T(128)}, u32[]{:S(2)}) copy-start(f32[64]{0:T(128)} %param.47) | copy-start | bytes 772
  48.8 135.7 %copy-start.20 = (f32[64]{0:T(128)S(1)}, f32[64]{0:T(128)}, u32[]{:S(2)}) copy-start(f32[64]{0:T(128)} %param.38) | copy-start | bytes 772
  48.9 135.7 %copy-start.21 = (f32[64]{0:T(128)S(1)}, f32[64]{0:T(128)}, u32[]{:S(2)}) copy-start(f32[64]{0:T(128)} %param.46) | copy-start | bytes 772
  48.9 139.4 %copy-start.6 = (f32[64,512]{1,0:T(8,128)S(1)}, f32[64,512]{1,0:T(8,128)}, u32[]{:S(2)}) copy-start(f32[64,512]{1,0:T(8,128)} %param.40) | copy-start | bytes 393220
  48.9 140.2 %copy-start.7 = (f32[512,64]{0,1:T(8,128)S(1)}, f32[512,64]{0,1:T(8,128)}, u32[]{:S(2)}) copy-start(f32[512,64]{0,1:T(8,128)} %param.41) | copy-start | bytes 393220
  48.9 141.0 %copy-start.15 = (f32[128,64]{0,1:T(8,128)S(1)}, f32[128,64]{0,1:T(8,128)}, u32[]{:S(2)}) copy-start(f32[128,64]{0,1:T(8,128)} %param.45) | copy-start | bytes 98308
  48.9 141.7 %copy-start.12 = (f32[64,128]{1,0:T(8,128)S(1)}, f32[64,128]{1,0:T(8,128)}, u32[]{:S(2)}) copy-start(f32[64,128]{1,0:T(8,128)} %param.44) | copy-start | bytes 98308
  48.9 141.7 %copy-start.13 = (f32[64,128]{1,0:T(8,128)S(1)}, f32[64,128]{1,0:T(8,128)}, u32[]{:S(2)}) copy-start(f32[64,128]{1,0:T(8,128)} %param.43) | copy-start | bytes 98308
  48.9 141.7 %copy-start.14 = (f32[64,128]{1,0:T(8,128)S(1)}, f32[64,128]{1,0:T(8,128)}, u32[]{:S(2)}) copy-start(f32[64,128]{1,0:T(8,128)} %param.42) | copy-start | bytes 98308
  178.4 9.8 %all-to-all-start = ((f32[8,1,768]{2,1,0:T(1,128)}), f32[8,1,768]{2,1,0:T(1,128)S(1)}, u32[]{:S(2)}, u32[]{:S(2)}) async-start(f32[8,1,768]{2,1,0:T(1,128)} %broadcast_in_dim.3), calls=%async_computation | async-start | bytes 49152 | tf_op jit(solution)/shard_map/all_to_all | solution.py:31
  183.5 56.0 %all-gather.2.cloned.1.call-start = ((), (), s32[]{:S(2)}) async-start(), calls=%async_computation.1 | async-start | bytes 3620864 | tf_op jit(solution)/shard_map/all_gather | solution.py:49
  (2 other events, 2.5 us)
Sparse Core Ops, SparseCore 0:
  49.1 125.8 all-reduce.3
  193.2 46.2 all-gather.1
where the time goes:
time: 256 us; the launch traced here: 255 us
  waiting for transfers between devices  173 us (68%)
  local copies, waits for them, and re-layouts  53.3 us (21%)
  between operations  15.1 us (6%)
  other arithmetic  8.86 us (3%)
  starting transfers between devices  5.13 us (2%)
    unnamed x3, waiting for transfers between devices  124 us
    all_gather x1, waiting for transfers between devices, rows_first(): lax.all_gather(both, axis, axis=0, tiled=True)  46.4 us
    unnamed x59, local copies, waits for them, and re-layouts  17.4 us
    pad x1, local copies, waits for them, and re-layouts, one_scatter(): jnp.pad(lines, ((0, 0), (0, rows * 128 - lines.shape[1]))).reshape(-1, 128)  5.86 us
    another operation x4, local copies, waits for them, and re-layouts, one_scatter(): lines = jnp.concatenate([b.reshape(length, -1) for b in parts], axis=1)  5.46 us
  transfers between devices with their start and end apart: 3, of which 3 were waited for; matrix products, arithmetic and copies ran while one was open for 1% of the time, Pallas kernels for 0%

commit v1 on v0

v1 whole, which is shorter than its diff:
```python
import jax
import jax.numpy as jnp
from jax import lax
from jax.experimental import pallas as pl
from jax.experimental.pallas import tpu as pltpu
from jax.sharding import PartitionSpec as P

learn_rate = 0.025
hold_rate = 0.7

R = 16
B = 64
T = 776
SCALE = 8192.0
SCALE_VEC = 4096.0
COLS = ((0, 4), (4, 1), (5, 1), (6, 1), (7, 4), (11, 1))


def pack_kernel(up, down, query, key, value, mixed, norm, bias, out):
    def put(col, tile):
        for n in range(tile.shape[1] // 128):
            part = tile[:, n * 128 : n * 128 + 128] * SCALE
            at = (col + n) * B
            out[0, at : at + B, :] = part[:B]
            out[1, at : at + B, :] = part[B:]

    put(0, up[0])
    put(4, query[0])
    put(5, key[0])
    put(6, value[0])
    put(7, down[0].T)
    put(11, mixed[0].T)
    nv = norm[0:1, :] * SCALE_VEC
    bv = bias[0:1, :] * SCALE_VEC
    row = lax.broadcasted_iota(jnp.int32, (8, 128), 0)

    def vectors(n, b):
        n = jnp.broadcast_to(n, (8, 128))
        b = jnp.broadcast_to(b, (8, 128))
        return jnp.where(row == 0, n, jnp.where(row == 1, b, 0.0))

    out[0, 768:776, :] = vectors(nv, bv)
    out[1, 768:776, :] = vectors(pltpu.roll(nv, 64, 1), pltpu.roll(bv, 64, 1))


def pack(up, down, query, key, value, mixed, norm, bias):
    return pl.pallas_call(
        pack_kernel,
        grid=(8,),
        in_specs=[
            pl.BlockSpec((1, 128, 512), lambda i: (0, i, 0)),
            pl.BlockSpec((1, 512, 128), lambda i: (0, 0, i)),
            pl.BlockSpec((1, 128, 128), lambda i: (0, i, 0)),
            pl.BlockSpec((1, 128, 128), lambda i: (0, i, 0)),
            pl.BlockSpec((1, 128, 128), lambda i: (0, i, 0)),
            pl.BlockSpec((1, 128, 128), lambda i: (0, 0, i)),
            pl.BlockSpec((1, 128), lambda i: (0, i)),
            pl.BlockSpec((1, 128), lambda i: (0, i)),
        ],
        out_specs=pl.BlockSpec((2, T, 128), lambda i: (i, 0, 0)),
        out_shape=jax.ShapeDtypeStruct((R, T, 128), jnp.float32),
        name="pack",
    )(up, down, query, key, value, mixed, norm, bias)


def norms_kernel(summed, p_up, p_query, p_key, p_value, p_down, p_mixed, mean, part):
    lane = lax.broadcasted_iota(jnp.int32, (B, 128), 1)
    params = (p_up, p_query, p_key, p_value, p_down, p_mixed)
    table = jnp.zeros((B, 128), jnp.float32)
    for m, (col, n) in enumerate(COLS):
        squares = jnp.zeros((B, 128), jnp.float32)
        own = jnp.zeros((B, 128), jnp.float32)
        for k in range(n):
            at = (col + k) * B
            total = summed[at : at + B, :] * (R**-0.5 / SCALE)
            mean[at : at + B, :] = total
            squares = squares + total * total
            p = params[m][:, k * 128 : k * 128 + 128]
            own = own + p * p
        s = jnp.sum(squares, axis=1, keepdims=True)
        o = jnp.sum(own, axis=1, keepdims=True)
        table = jnp.where(lane == m, o, jnp.where(lane == 8 + m, s, table))
    mean[768:776, :] = summed[768:776, :] * (R**-0.5 / SCALE_VEC)
    table = jnp.concatenate([table, jnp.zeros((128 - B, 128), jnp.float32)], axis=0)
    part[...] = table.T[:16, :]


def norms(summed, *params):
    return pl.pallas_call(
        norms_kernel,
        out_shape=(
            jax.ShapeDtypeStruct((T, 128), jnp.float32),
            jax.ShapeDtypeStruct((16, 128), jnp.float32),
        ),
        name="norms",
    )(summed, *params)


def update_kernel(parts, mean, *refs):
    params, states = refs[:8], refs[8:16]
    nexts, news, half = refs[16:24], refs[24:32], refs[32]
    sums = parts[0]
    for d in range(1, parts.shape[0]):
        sums = sums + parts[d]
    ratio = jnp.sqrt(sums[:8]) * lax.rsqrt(sums[8:16] + 1e-06)
    ratio = jnp.concatenate([ratio, jnp.zeros((120, 128), jnp.float32)], axis=0).T[:B, :]

    def step(m, param, state):
        new = hold_rate * state + (1.0 - hold_rate) * m * m
        return param - learn_rate * m * lax.rsqrt(new + 1e-06), new

    for i, (col, n) in enumerate(COLS):
        r = ratio[:, i : i + 1]
        for k in range(n):
            at = (col + k) * B
            lanes = slice(k * 128, k * 128 + 128)
            nxt, new = step(mean[at : at + B, :] * r, params[i][:, lanes], states[i][:, lanes])
            nexts[i][:, lanes] = nxt
            news[i][:, lanes] = new
            half[at : at + B, :] = nxt.astype(jnp.bfloat16)
    both = []
    for j in range(2):
        nxt, new = step(mean[768 + j : 769 + j, :B], params[6 + j][...], states[6 + j][...])
        nexts[6 + j][...] = nxt
        news[6 + j][...] = new
        both.append(jnp.concatenate([nxt, nxt], axis=1))
    row = lax.broadcasted_iota(jnp.int32, (8, 128), 0)
    n = jnp.broadcast_to(both[0], (8, 128))
    b = jnp.broadcast_to(both[1], (8, 128))
    half[768:776, :] = jnp.where(row == 0, n, jnp.where(row == 1, b, 0.0)).astype(jnp.bfloat16)


def update(parts, mean, params, states):
    shapes = [jax.ShapeDtypeStruct(p.shape, jnp.float32) for p in params]
    out = pl.pallas_call(
        update_kernel,
        out_shape=(*shapes, *shapes, jax.ShapeDtypeStruct((T, 128), jnp.bfloat16)),
        name="update",
    )(parts, mean, *params, *states)
    return out[:8], out[8:16], out[16]


def unpack_kernel(recv, up, query, key, value, down, mixed, norm, bias):
    def get(col):
        at = col * B
        return jnp.concatenate([recv[0, at : at + B, :], recv[1, at : at + B, :]], axis=0)

    for k in range(4):
        up[:, k * 128 : k * 128 + 128] = get(k)
    query[...] = get(4)
    key[...] = get(5)
    value[...] = get(6)
    for k in range(4):
        down[k * 128 : k * 128 + 128, :] = get(7 + k).T
    mixed[...] = get(11).T
    lane = lax.broadcasted_iota(jnp.int32, (8, 128), 1)
    last = jnp.where(
        lane < B, recv[0, 768:776, :].astype(jnp.float32), recv[1, 768:776, :].astype(jnp.float32)
    )
    norm[...] = last[0:1].astype(jnp.bfloat16)
    bias[...] = last[1:2].astype(jnp.bfloat16)


def unpack(recv):
    bf16 = jnp.bfloat16
    return pl.pallas_call(
        unpack_kernel,
        grid=(8,),
        in_specs=[pl.BlockSpec((2, T, 128), lambda i: (i, 0, 0))],
        out_specs=(
            pl.BlockSpec((128, 512), lambda i: (i, 0)),
            pl.BlockSpec((128, 128), lambda i: (i, 0)),
            pl.BlockSpec((128, 128), lambda i: (i, 0)),
            pl.BlockSpec((128, 128), lambda i: (i, 0)),
            pl.BlockSpec((512, 128), lambda i: (0, i)),
            pl.BlockSpec((128, 128), lambda i: (0, i)),
            pl.BlockSpec((1, 128), lambda i: (0, i)),
            pl.BlockSpec((1, 128), lambda i: (0, i)),
        ),
        out_shape=(
            jax.ShapeDtypeStruct((1024, 512), bf16),
            jax.ShapeDtypeStruct((1024, 128), bf16),
            jax.ShapeDtypeStruct((1024, 128), bf16),
            jax.ShapeDtypeStruct((1024, 128), bf16),
            jax.ShapeDtypeStruct((512, 1024), bf16),
            jax.ShapeDtypeStruct((128, 1024), bf16),
            jax.ShapeDtypeStruct((1, 1024), bf16),
            jax.ShapeDtypeStruct((1, 1024), bf16),
        ),
        name="unpack",
    )(recv)


def local(*args):
    slopes, params, states = args[:8], args[8:16], args[16:24]

    def inner(xs):
        up, down, query, key, value, mixed, norm, bias = xs
        return up, query, key, value, down.T, mixed.T, norm[None], bias[None]

    params, states = inner(params), inner(states)
    packed = pack(*slopes)
    recv = lax.all_to_all(packed.astype(jnp.float16), "replica", 0, 0, tiled=True)
    mean, part = norms(recv.astype(jnp.float32).sum(axis=0), *params[:6])
    copies = jnp.broadcast_to(part, (lax.axis_size("model"), *part.shape))
    parts = lax.all_to_all(copies, "model", 0, 0, tiled=True)
    nexts, news, half = update(parts, mean, params, states)
    copies = jnp.broadcast_to(half, (R, *half.shape))
    gathered = lax.all_to_all(copies, "replica", 0, 0, tiled=True)
    up, query, key, value, down, mixed, norm, bias = unpack(gathered)

    def outer(xs):
        up, query, key, value, down, mixed, norm, bias = xs
        return up, down.T, query, key, value, mixed.T, norm[0], bias[0]

    return (
        up, down, query, key, value, mixed, norm[0], bias[0],
        *outer(nexts),
        *outer(news),
    )


def solution(mesh):
    cut = [P("replica", "model"), P("model", "replica")] + [P("replica", "model")] * 3
    cut += [P("model", "replica"), P("replica"), P("replica")]
    slope = [P("replica", None, "model"), P("replica", "model", None)] + [P("replica", None, "model")] * 3
    slope += [P("replica", "model", None), P("replica", None), P("replica", None)]
    half = [P(None, "model"), P("model", None)] + [P(None, "model")] * 3 + [P("model", None), P(), P()]
    return jax.shard_map(
        local,
        mesh=mesh,
        in_specs=(*slope, *cut, *cut),
        out_specs=(*half, *cut, *cut),
        check_vma=False,
    )
```

time: 256 us -> 131 us (0.51)
  waiting for transfers between devices: 173 us -> 0 us
  blocking collectives: 0 us -> 101 us
  local copies, waits for them, and re-layouts: 53.3 us -> 2.04 us
  Pallas kernels: 0 us -> 18.9 us
  between operations: 15.1 us -> 0.68 us
  starting transfers between devices: 5.13 us -> 0 us
    unnamed x3 -> x0, waiting for transfers between devices: 124 us -> none
    all_to_all x0 -> x3, blocking collectives: none -> 101 us  [the longest x1 47.7 us: local(): lax.all_to_all(packed.astype(jnp.float16), 'replica', 0, 0, tiled=True)]
    all_gather x1 -> x0, waiting for transfers between devices: 46.4 us -> none  [rows_first(): lax.all_gather(both, axis, axis=0, tiled=True)]
    pallas_call x0 -> x4, Pallas kernels: none -> 18.9 us  [the longest x1 8.16 us: pack(): pl.pallas_call(pack_kernel, grid=(8,), in_specs=[pl.BlockSpec((1, 128, 51...]
    unnamed x59 -> x0, local copies, waits for them, and re-layouts: 17.4 us -> none
    reshape x11 -> x0, local copies, waits for them, and re-layouts: 10.8 us -> none  [the longest x1 5.02 us: one_scatter(): jnp.pad(lines, ((0, 0), (0, rows * 128 - lines.shape[1]))).reshape(-1, 128)]
    transpose x4 -> x0, local copies, waits for them, and re-layouts: 8.83 us -> none  [the longest x2 4.76 us: rows_first(): finished.append(jnp.moveaxis(section, 0, dim))]
    pad x1 -> x0, local copies, waits for them, and re-layouts: 5.86 us -> none  [one_scatter(): jnp.pad(lines, ((0, 0), (0, rows * 128 - lines.shape[1]))).reshape(-1, 128)]
  transfers between devices with their start and end apart: 3 -> 0, of which waited for: 3 -> 0; matrix products, arithmetic and copies ran while one was open for 1% -> 0% of each run, Pallas kernels for 0% -> 0%
where the time goes in v1:
time: 131 us; the launch traced here: 130 us
  blocking collectives  101 us (77%)
  Pallas kernels  18.9 us (14%)
  other arithmetic  6.94 us (5%)
  local copies, waits for them, and re-layouts  2.04 us (2%)
    all_to_all x1, blocking collectives, local(): lax.all_to_all(packed.astype(jnp.float16), 'replica', 0, 0, tiled=True)  47.7 us
    all_to_all x1, blocking collectives, local(): gathered = lax.all_to_all(copies, 'replica', 0, 0, tiled=True)  42.6 us
    all_to_all x1, blocking collectives, local(): parts = lax.all_to_all(copies, 'model', 0, 0, tiled=True)  10.8 us
    pallas_call x1, Pallas kernels, pack(): pl.pallas_call(pack_kernel, grid=(8,), in_specs=[pl.BlockSpec((1, 128, 51...  8.16 us
    pallas_call x1, Pallas kernels, unpack(): pl.pallas_call(unpack_kernel, grid=(8,), in_specs=[pl.BlockSpec((2, T, 12...  6.13 us
    convert_element_type x1, other arithmetic, local(): packed.astype(jnp.float16)  3.21 us

profile of v1, /device:TPU:1, one launch (start us, length us, event | category | flops | bytes accessed | tf_op | source)
XLA Modules:
  0.0 129.6 jit_solution(10431877650471421121)
XLA Ops:
  0.7 8.2 %pack.1 = f32[16,776,128]{2,1,0:T(8,128)} custom-call(f32[1,1024,512]{2,1,0:T(8,128)} %up.1, f32[1,512,1024]{2,1,0:T(8,128)} %down.1, f32[1,1024,128]{2,1,0:T(8,128)} %query.1, f32[1,1024,128]{2,1,0:T(8,128)} %key.1, f32[1,1024,128]{2,1,0:T(8,128)} %value.1, f32[1,128,1024]{2,1,0:T(8,128)} %mixed.1, f32[1,1024]{1,0:T(1,128)} %norm.1, f32[1,1024]{1,0:T(1,128)} %bias.1), custom_call_target="tpu_custom_call" | custom-call | tf_op jit(solution)/shard_map/pack/pallas_call | solution.py:47
  8.8 3.2 %convert_element_type.6 = f16[16,776,128]{2,1,0:T(8,128)(2,1)S(1)} convert(f32[16,776,128]{2,1,0:T(8,128)} %pack.1) | non-fusion elementwise | flops 1589248 | bytes 9535488 | tf_op jit(solution)/shard_map/convert_element_type | solution.py:203
  12.0 47.7 %all_to_all.15 = f16[16,776,128]{2,1,0:T(8,128)(2,1)S(1)} all-to-all(f16[16,776,128]{2,1,0:T(8,128)(2,1)S(1)} %convert_element_type.6), channel_id=1, replica_groups=mesh['replica'=16,'model'=8] {'replica'}, dimensions={0} | all-to-all | bytes 6356992 | tf_op jit(solution)/shard_map/all_to_all | solution.py:203
  59.7 1.2 convert_reduce_fusion.summed
  60.9 2.1 %norms.1 = (f32[776,128]{1,0:T(8,128)}, f32[16,128]{1,0:T(8,128)}) custom-call(f32[776,128]{1,0:T(8,128)} %convert_reduce_fusion.summed, f32[64,512]{1,0:T(8,128)} %refs_0_.1, f32[64,128]{1,0:T(8,128)} %refs_1_.1, f32[64,128]{1,0:T(8,128)} %refs_2_.1, f32[64,128]{1,0:T(8,128)} %refs_3_.1, f32[64,512]{1,0:T(8,128)} %bitcast.16, f32[64,128]{1,0:T(8,128)} %bitcast.19), custom_call_target="tpu_custom_call" | custom-call | tf_op jit(solution)/shard_map/norms/pallas_call | solution.py:89
  62.9 0.7 broadcast_in_dim.18
  63.6 10.8 %all_to_all.16.parts = f32[8,16,128]{2,1,0:T(8,128)} all-to-all(f32[8,16,128]{2,1,0:T(8,128)S(1)} %broadcast_in_dim.18), channel_id=1, replica_groups=mesh['replica'=16,'model'=8] {'model'}, dimensions={0} | all-to-all | bytes 131072 | tf_op jit(solution)/shard_map/all_to_all | solution.py:206
  74.5 2.5 %update.1 = (f32[64,512]{1,0:T(8,128)}, f32[64,128]{1,0:T(8,128)}, f32[64,128]{1,0:T(8,128)}, f32[64,128]{1,0:T(8,128)}, f32[64,512]{1,0:T(8,128)}, /*index=5*/f...) custom-call(f32[8,16,128]{2,1,0:T(8,128)} %all_to_all.16.parts, ...), custom_call_target="tpu_custom_call" | custom-call | tf_op jit(solution)/shard_map/update/pallas_call | solution.py:135
  77.0 1.3 %broadcast_in_dim.23 = bf16[16,776,128]{2,1,0:T(8,128)(2,1)S(1)} broadcast(bf16[776,128]{1,0:T(8,128)(2,1)} %get-tuple-element.53), dimensions={1,2} | broadcast | bytes 3377152 | tf_op jit(solution)/shard_map/broadcast_in_dim | solution.py:208
  78.3 42.6 %all_to_all.17.recv = bf16[16,776,128]{2,1,0:T(8,128)(2,1)} all-to-all(bf16[16,776,128]{2,1,0:T(8,128)(2,1)S(1)} %broadcast_in_dim.23), channel_id=1, replica_groups=mesh['replica'=16,'model'=8] {'replica'}, dimensions={0} | all-to-all | bytes 6356992 | tf_op jit(solution)/shard_map/all_to_all | solution.py:209
  120.9 6.1 %unpack.1 = (bf16[1024,512]{1,0:T(8,128)(2,1)}, bf16[1024,128]{1,0:T(8,128)(2,1)}, bf16[1024,128]{1,0:T(8,128)(2,1)}, bf16[1024,128]{1,0:T(8,128)(2,1)}, bf16[51...) custom-call(bf16[16,776,128]{2,1,0:T(8,128)(2,1)} %all_to_all.17.recv), custom_call_target="tpu_custom_call" | custom-call | tf_op jit(solution)/shard_map/unpack/pallas_call | solution.py:166
  127.1 1.3 reduce
  128.3 1.3 reduce.1
